TPU v7x, 32 devices: a whole 2x2x4 slice. The times are simulated.
32 devices in a mesh: expert: 4 (over z), shard: 8 (over y, x, core).
Axes of the slice: x: 2, y: 2, z: 4, core: 2. Of those that a mesh axis runs over, the one named last changes fastest.
Arguments:
- tokens: bfloat16 [768, 4096], P(('expert', 'shard')), may hold values from -0.19921875 to 0.19921875
- expert_ids: int32 [768, 2], P(('expert', 'shard')), may hold values from 0 to 3, all different within a row; in each aligned block of 24 rows (0 to 23, 24 to 47, ...) at most 16 rows name the same one
- weight_gate: bfloat16 [4, 4096, 8192], P('expert', None, 'shard'), may hold values from -0.09375 to 0.09375
- weight_up: bfloat16 [4, 4096, 8192], P('expert', None, 'shard'), may hold values from -0.09375 to 0.09375
- gate_pre: bfloat16 [4, 512, 8192], P('expert', None, 'shard'), may hold values from -8 to 8
- up_pre: bfloat16 [4, 512, 8192], P('expert', None, 'shard'), may hold values from -6 to 6
- hidden_grad: bfloat16 [4, 512, 8192], P('expert', None, 'shard'), may hold values from -6 to 6
Outputs:
- token_grad: bfloat16 [768, 4096], P(('expert', 'shard'))
- gate_weight_grad: float32 [4, 4096, 8192], P('expert', None, 'shard')
- up_weight_grad: float32 [4, 4096, 8192], P('expert', None, 'shard')
Inputs may be any that keep to these rules, and one draw needn't show every extreme that they name: `expert_ids`: each token names 2 different experts. Among the tokens of one device no expert is named more than 16 times, and in every draw some device names some expert exactly 16 times.
All inputs are finite; a program needn't handle non-finite values.
Results may differ from a plain program's by a relative error of at most 0.02.
Values may be sent and summed in bfloat16 or wider, within the bound.
A program may use at most 192 MiB of HBM per device.

v0:
```python
import functools
import jax
import jax.numpy as jnp
from jax import lax
from jax.experimental import pallas as pl
from jax.experimental.pallas import tpu as pltpu
from jax.sharding import PartitionSpec as P

MESH = pl.DeviceIdType.MESH
CHUNKS = 4
COPIES = 21


def swiglu_grads(gate_values, up_values, hidden_cotangent):
    gate_float = gate_values.astype(jnp.float32)
    up_float = up_values.astype(jnp.float32)
    cotangent = hidden_cotangent.astype(jnp.float32)
    sigmoid_gate = jax.nn.sigmoid(gate_float)
    gate_grad = (
        cotangent * up_float * sigmoid_gate * (1.0 + gate_float * (1.0 - sigmoid_gate))
    ).astype(jnp.bfloat16)
    up_grad = (cotangent * gate_float * sigmoid_gate).astype(jnp.bfloat16)
    return (gate_grad, up_grad)


def slot_table(expert_ids, groups, capacity):
    token_count = expert_ids.shape[0]
    choices_per = expert_ids.shape[1]
    labels = lax.broadcasted_iota(jnp.int32, (1, 1, groups), 2)
    one_hot = (expert_ids[:, :, None] == labels).astype(jnp.int32)
    flat_hits = one_hot.reshape(token_count * choices_per, groups)
    earlier = jnp.cumsum(flat_hits, axis=0) - flat_hits
    slot_index = jnp.sum(flat_hits * earlier, axis=1).reshape(token_count, choices_per)
    slot_labels = lax.broadcasted_iota(jnp.int32, (1, 1, 1, capacity), 3)
    slot_hits = one_hot[:, :, :, None] * (slot_index[:, :, None, None] == slot_labels).astype(
        jnp.int32
    )
    selection = jnp.sum(slot_hits, axis=1).reshape(token_count, groups * capacity)
    return selection.astype(jnp.bfloat16)


def rows_inner(left_rows, right_rows):
    return lax.dot_general(
        left_rows, right_rows, (((0,), (0,)), ((), ())), preferred_element_type=jnp.float32
    )


def times_transposed(left_rows, weights):
    return lax.dot_general(
        left_rows, weights, (((1,), (1,)), ((), ())), preferred_element_type=jnp.float32
    )


def on_device_general(tokens, expert_ids, weight_gate, weight_up, gate_pre, up_pre, hidden_grad):
    groups = lax.axis_size("expert")
    shards = lax.axis_size("shard")
    model_width = tokens.shape[1]
    capacity = gate_pre.shape[1] // (groups * shards)
    selection = slot_table(expert_ids, groups, capacity)
    outgoing = rows_inner(selection, tokens).astype(jnp.bfloat16)
    gate_grad, up_grad = swiglu_grads(gate_pre[0], up_pre[0], hidden_grad[0])
    gate_matrix = weight_gate[0]
    up_matrix = weight_up[0]
    arrived = lax.all_to_all(
        outgoing.reshape(groups, capacity, model_width),
        "expert",
        split_axis=0,
        concat_axis=0,
        tiled=True,
    )
    block_rows = lax.all_gather(
        arrived.reshape(groups * capacity, model_width), "shard", axis=0, tiled=True
    )
    gate_rows = gate_grad
    up_rows = up_grad
    gate_wgrad = rows_inner(block_rows, gate_rows)
    up_wgrad = rows_inner(block_rows, up_rows)
    gate_rows = gate_grad
    up_rows = up_grad
    summed = lax.psum_scatter(
        (times_transposed(gate_rows, gate_matrix) + times_transposed(up_rows, up_matrix)).astype(
            jnp.bfloat16
        ),
        "shard",
        scatter_dimension=0,
        tiled=True,
    )
    outbound = summed.reshape(groups, capacity, model_width)
    returned = lax.all_to_all(outbound, "expert", split_axis=0, concat_axis=0, tiled=True)
    returned = returned.reshape(groups * capacity, model_width)
    token_grad = times_transposed(selection, returned.T).astype(jnp.bfloat16)
    return (token_grad, gate_wgrad[None], up_wgrad[None])


def slot_choice(expert_ids, groups, capacity):
    token_count = expert_ids.shape[0]
    lanes = lax.broadcasted_iota(jnp.int32, (token_count, groups * capacity), 1)
    expert, slot = lanes // capacity, lanes % capacity
    named = jnp.logical_or(expert_ids[:, 0:1] == expert, expert_ids[:, 1:2] == expert)
    hits = jnp.where(named, 1.0, 0.0)
    above = lax.broadcasted_iota(jnp.int32, (token_count, token_count), 0)
    below = lax.broadcasted_iota(jnp.int32, (token_count, token_count), 1)
    before = jnp.where(below < above, 1.0, 0.0)
    earlier = jnp.dot(before, hits, preferred_element_type=jnp.float32)
    chosen = jnp.logical_and(named, earlier == slot.astype(jnp.float32))
    return jnp.where(chosen, 1.0, 0.0).astype(jnp.bfloat16)


def paced(step):
    early = jnp.where(step < 3, step, -1)
    middle = jnp.where(jnp.logical_and(step >= 4, step % 2 == 0), step // 2 + 1, early)
    return jnp.where(step > 8, step - 3, middle)


def exchange_kernel(
    groups, capacity, chunks, width,
    tokens, expert_ids, weight_gate, weight_up, gate_pre, up_pre, hidden_grad,
    returned_out, block_rows, gate_out, up_out,
    token_buf, outgoing, gate_w, up_w, pre, gate_rows, up_rows, block, partial, from_core, total, from_diag,
    from_near, leaving, returned, load_sem, store_sem, local_sem, send_sem, recv_sem,
):
    e = lax.axis_index("expert")
    q = lax.axis_index("shard")
    core, x, y = q % 2, (q // 2) % 2, q // 4
    sib = q + 1 - 2 * core
    xn = q + 2 - 4 * x
    yn = q + 4 - 8 * y
    dg = xn + 4 - 8 * y
    rows = groups * capacity
    half = rows // 2
    slots = gate_rows.shape[0]
    part = slots // 4

    def pre_load(i, source):
        return pltpu.make_async_copy(source.at[0], pre.at[i], load_sem.at[2 * chunks + i])

    def weight_load(i, c, source, target):
        return pltpu.make_async_copy(
            source.at[0, pl.ds(pl.multiple_of(c * width, width), width), :],
            target.at[c], load_sem.at[2 * c + i],
        )

    def columns(c):
        return pl.ds(pl.multiple_of(c * width, width), width)

    def span(start, size):
        return pl.ds(pl.multiple_of(start, size), size)

    def held(c, start, size):
        return block.at[c, span(start, size), :]

    def chip_rows(c, device, low, size):
        return total.at[c, span(device // 2 * rows + low, size), :]

    def other(k):
        return (e + k) % groups

    def target(k):
        if k < 3:
            return (other(k + 1), q)
        if k >= 18:
            return (other(k - 17), q)
        if k in (3, 7, 12, 14, 16):
            return (e, xn)
        if k in (4, 6, 13, 15, 17):
            return (e, yn)
        return (e, sib)

    def copy(k, c):
        if k < 3:
            source = outgoing.at[other(k + 1), :, columns(c)]
            to = held(c, q * rows + e * capacity, capacity)
        elif k < 6:
            source = to = held(c, q * rows, rows)
        elif k == 6:
            source = to = held(c, xn * rows, half)
        elif k == 7:
            source = to = held(c, yn * rows + half, half)
        elif k < 11:
            source = to = held(c, (xn, yn, dg)[k - 8] * rows, rows)
        elif k == 11:
            source, to = partial.at[c, 1 - core], from_core.at[c]
        elif k == 12:
            source, to = chip_rows(c, dg, 0, half), from_diag.at[c, 0]
        elif k == 13:
            source, to = chip_rows(c, dg, half, half), from_diag.at[c, 1]
        elif k == 14:
            source, to = chip_rows(c, xn, 0, half), from_near.at[c, 0, 0]
        elif k == 15:
            source, to = chip_rows(c, yn, half, half), from_near.at[c, 1, 1]
        elif k == 16:
            source, to = chip_rows(c, xn, half, half), from_near.at[c, 0, 1]
        elif k == 17:
            source, to = chip_rows(c, yn, 0, half), from_near.at[c, 1, 0]
        else:
            source = leaving.at[c, span(other(k - 17) * capacity, capacity), :]
            to = returned.at[c, span(e * capacity, capacity), :]
        return pltpu.make_async_remote_copy(
            src_ref=source, dst_ref=to, send_sem=send_sem.at[c, k], recv_sem=recv_sem.at[c, k],
            device_id=target(k), device_id_type=MESH,
        )

    def landing(k, c):
        if k < 3:
            return held(c, q * rows + (e + groups - k - 1) % groups * capacity, capacity)
        if k < 6:
            return held(c, (xn, yn, sib)[k - 3] * rows, rows)
        if k == 6:
            return held(c, dg * rows, half)
        if k == 7:
            return held(c, dg * rows + half, half)
        if k < 11:
            return held(c, (sib + (xn, yn, dg)[k - 8] - q) * rows, rows)
        if k >= 18:
            source = (e + groups - k + 17) % groups
            return returned.at[c, span(source * capacity, capacity), :]
        return {
            11: from_core.at[c], 12: from_diag.at[c, 0], 13: from_diag.at[c, 1],
            14: from_near.at[c, 0, 0], 15: from_near.at[c, 1, 1],
            16: from_near.at[c, 0, 1], 17: from_near.at[c, 1, 0],
        }[k]

    def arrive(k, c):
        place = landing(k, c)
        pltpu.make_async_remote_copy(
            src_ref=place, dst_ref=place, send_sem=send_sem.at[c, k], recv_sem=recv_sem.at[c, k],
            device_id=target(k), device_id_type=MESH,
        ).wait_recv()

    def own_rows(c):
        return pltpu.make_async_copy(
            outgoing.at[e, :, columns(c)], held(c, q * rows + e * capacity, capacity),
            local_sem.at[c],
        )

    def rows_out(c):
        return pltpu.make_async_copy(
            block.at[c], block_rows.at[:, columns(c)], store_sem.at[c]
        )

    def returns_out(c):
        return pltpu.make_async_copy(
            returned.at[c], returned_out.at[:, columns(c)], store_sem.at[chunks + 2 + c]
        )

    def grads_out(i):
        return pltpu.make_async_copy(
            (gate_rows, up_rows)[i], (gate_out, up_out)[i], store_sem.at[chunks + i]
        )

    token_load = pltpu.make_async_copy(tokens, token_buf, load_sem.at[2 * chunks + 3])
    token_load.start()
    for i, source in enumerate((gate_pre, up_pre, hidden_grad)):
        pre_load(i, source).start()

    @pl.loop(0, chunks)
    def _(c):
        weight_load(0, c, weight_gate, gate_w).start()
        weight_load(1, c, weight_up, up_w).start()

    barrier = pltpu.get_barrier_semaphore()
    for device in ((other(1), q), (other(2), q), (other(3), q), (e, sib), (e, xn), (e, yn)):
        pl.semaphore_signal(barrier, inc=1, device_id=device, device_id_type=MESH)
    selection = slot_choice(expert_ids[...], groups, capacity)
    token_load.wait()
    for c in range(chunks):
        here = slice(c * width, (c + 1) * width)
        picked = rows_inner(selection, token_buf[:, here]).astype(jnp.bfloat16)
        for group in range(groups):
            outgoing[group, :, here] = picked[group * capacity : (group + 1) * capacity]
    pl.semaphore_wait(barrier, 6)

    @pl.loop(0, chunks)
    def _(c):
        own_rows(c).start()
        for k in (1, 0, 2):
            copy(k, c).start()

    for i, source in enumerate((gate_pre, up_pre, hidden_grad)):
        pre_load(i, source).wait()

    step_rows = 32

    @pl.loop(0, slots // step_rows)
    def _(i):
        here = span(i * step_rows, step_rows)
        gate_grad, up_grad = swiglu_grads(pre[0, here, :], pre[1, here, :], pre[2, here, :])
        gate_rows[here, :] = gate_grad
        up_rows[here, :] = up_grad

    for i in range(2):
        grads_out(i).start()

    def spread(c):
        own_rows(c).wait()
        for k in (0, 1, 2):
            arrive(k, c)
        for k in (3, 4, 5):
            copy(k, c).start()

    def forward(c):
        arrive(3, c)
        copy(6, c).start()
        copy(8, c).start()
        arrive(4, c)
        copy(7, c).start()
        copy(9, c).start()

    def far(c):
        arrive(6, c)
        arrive(7, c)
        copy(10, c).start()

    def gathered(c):
        for k in (5, 8, 9, 10):
            arrive(k, c)
        rows_out(c).start()

    def multiply(c):
        weight_load(0, c, weight_gate, gate_w).wait()
        weight_load(1, c, weight_up, up_w).wait()
        term = times_transposed(gate_rows[...], gate_w[c]) + times_transposed(up_rows[...], up_w[c])
        term = term.astype(jnp.bfloat16)
        for chip in range(slots // (2 * rows)):
            for side in range(2):
                low = (2 * chip + side) * rows
                partial[c, side, chip * rows : (chip + 1) * rows, :] = term[low : low + rows]
        copy(11, c).start()

    def pair_sum(c):
        arrive(11, c)
        both = partial[c, core].astype(jnp.float32) + from_core[c].astype(jnp.float32)
        total[c] = both.astype(jnp.bfloat16)
        for k in (12, 13, 14, 15):
            copy(k, c).start()

    def near_sum(c):
        for k, side, device, low in ((12, 0, yn, 0), (13, 1, xn, half)):
            arrive(k, c)
            place = span(device // 2 * rows + low, half)
            added = total[c, place, :].astype(jnp.float32) + from_diag[c, side].astype(jnp.float32)
            total[c, place, :] = added.astype(jnp.bfloat16)
            copy(17 if side == 0 else 16, c).start()

    def own_sum(c):
        for k in (14, 15, 16, 17):
            arrive(k, c)
        for low in range(2):
            place = span(q // 2 * rows + low * half, half)
            added = total[c, place, :].astype(jnp.float32)
            added = added + from_near[c, 0, low].astype(jnp.float32)
            added = added + from_near[c, 1, low].astype(jnp.float32)
            leaving[c, low * half : (low + 1) * half, :] = added.astype(jnp.bfloat16)
        mine = span(e * capacity, capacity)
        returned[c, mine, :] = leaving[c, mine, :]
        for k in (19, 18, 20):
            copy(k, c).start()

    def combine(c):
        for k in (18, 19, 20):
            arrive(k, c)
        returns_out(c).start()

    stages = (
        (spread, 0, paced), (forward, 1, paced), (pair_sum, 1, None), (near_sum, 2, None),
        (far, 2, paced), (own_sum, 3, None), (multiply, 0, None), (gathered, 3, paced),
        (combine, 4, None),
    )

    @pl.loop(0, chunks + 4)
    def _(step):
        for stage, lag, pace in stages:
            c = step - lag

            @pl.when(jnp.logical_and(c >= 0, c < chunks))
            def _():
                stage(c)

    @pl.loop(0, chunks)
    def _(c):
        for k in range(COPIES):
            copy(k, c).wait_send()
        rows_out(c).wait()
        returns_out(c).wait()

    for i in range(2):
        grads_out(i).wait()


def weight_grad_kernel(
    groups, capacity, expert_ids, returned, block_rows, gate_rows, up_rows,
    token_grad, gate_wgrad, up_wgrad, selection,
):
    @pl.when(pl.program_id(0) == 0)
    def _():
        selection[...] = slot_choice(expert_ids[...], groups, capacity)

    left = block_rows[...]
    gate_wgrad[0] = rows_inner(left, gate_rows[...])
    up_wgrad[0] = rows_inner(left, up_rows[...])
    token_grad[...] = jnp.dot(
        selection[...], returned[...], preferred_element_type=jnp.float32
    ).astype(jnp.bfloat16)


def on_device(tokens, expert_ids, weight_gate, weight_up, gate_pre, up_pre, hidden_grad):
    groups = lax.axis_size("expert")
    shards = lax.axis_size("shard")
    token_count, model_width = tokens.shape
    slots, hidden = gate_pre.shape[1:]
    capacity = slots // (groups * shards)
    rows = groups * capacity
    chunks = CHUNKS
    width = model_width // chunks
    bf16 = jnp.bfloat16
    in_vmem = pl.BlockSpec(memory_space=pltpu.VMEM)
    anywhere = pl.BlockSpec(memory_space=pl.ANY)
    returned, block_rows, gate_rows, up_rows = pl.pallas_call(
        functools.partial(exchange_kernel, groups, capacity, chunks, width),
        out_shape=(
            jax.ShapeDtypeStruct((rows, model_width), bf16),
            jax.ShapeDtypeStruct((slots, model_width), bf16),
            jax.ShapeDtypeStruct((slots, hidden), bf16),
            jax.ShapeDtypeStruct((slots, hidden), bf16),
        ),
        in_specs=[anywhere, in_vmem] + [anywhere] * 5,
        out_specs=(anywhere, anywhere, anywhere, anywhere),
        scratch_shapes=[
            pltpu.VMEM((token_count, model_width), bf16),
            pltpu.VMEM((groups, capacity, model_width), bf16),
            pltpu.VMEM((chunks, width, hidden), bf16),
            pltpu.VMEM((chunks, width, hidden), bf16),
            pltpu.VMEM((3, slots, hidden), bf16),
            pltpu.VMEM((slots, hidden), bf16),
            pltpu.VMEM((slots, hidden), bf16),
            pltpu.VMEM((chunks, slots, width), bf16),
            pltpu.VMEM((chunks, 2, slots // 2, width), bf16),
            pltpu.VMEM((chunks, slots // 2, width), bf16),
            pltpu.VMEM((chunks, slots // 2, width), bf16),
            pltpu.VMEM((chunks, 2, rows // 2, width), bf16),
            pltpu.VMEM((chunks, 2, 2, rows // 2, width), bf16),
            pltpu.VMEM((chunks, rows, width), bf16),
            pltpu.VMEM((chunks, rows, width), bf16),
            pltpu.SemaphoreType.DMA((2 * chunks + 4,)),
            pltpu.SemaphoreType.DMA((2 * chunks + 2,)),
            pltpu.SemaphoreType.DMA((chunks,)),
            pltpu.SemaphoreType.DMA((chunks, COPIES)),
            pltpu.SemaphoreType.DMA((chunks, COPIES)),
        ],
        compiler_params=pltpu.CompilerParams(
            collective_id=0, has_side_effects=True, vmem_limit_bytes=60 * 1024 * 1024
        ),
    )(tokens, expert_ids, weight_gate, weight_up, gate_pre, up_pre, hidden_grad)
    tile = min(1024, model_width)
    wgrad_shape = jax.ShapeDtypeStruct((1, model_width, hidden), jnp.float32)
    token_grad, gate_wgrad, up_wgrad = pl.pallas_call(
        functools.partial(weight_grad_kernel, groups, capacity),
        grid=(model_width // tile,),
        out_shape=(jax.ShapeDtypeStruct((token_count, model_width), bf16), wgrad_shape, wgrad_shape),
        in_specs=[
            pl.BlockSpec(expert_ids.shape, lambda i: (0, 0)),
            pl.BlockSpec((rows, tile), lambda i: (0, i)),
            pl.BlockSpec((slots, tile), lambda i: (0, i)),
            pl.BlockSpec((slots, hidden), lambda i: (0, 0)),
            pl.BlockSpec((slots, hidden), lambda i: (0, 0)),
        ],
        out_specs=(
            pl.BlockSpec((token_count, tile), lambda i: (0, i)),
            pl.BlockSpec((1, tile, hidden), lambda i: (0, i, 0)),
            pl.BlockSpec((1, tile, hidden), lambda i: (0, i, 0)),
        ),
        scratch_shapes=[pltpu.VMEM((token_count, rows), bf16)],
        compiler_params=pltpu.CompilerParams(vmem_limit_bytes=63 * 1024 * 1024),
    )(expert_ids, returned, block_rows, gate_rows, up_rows)
    return (token_grad, gate_wgrad, up_wgrad)


def solution(mesh):
    placed = (
        P(("expert", "shard"), None),
        P(("expert", "shard"), None),
        P("expert", None, "shard"),
        P("expert", None, "shard"),
        P("expert", None, "shard"),
        P("expert", None, "shard"),
        P("expert", None, "shard"),
    )
    small = mesh.shape["shard"] == 8 and mesh.shape["expert"] == 4
    return jax.shard_map(
        on_device if small else on_device_general,
        mesh=mesh,
        in_specs=placed,
        out_specs=(
            P(("expert", "shard"), None),
            P("expert", None, "shard"),
            P("expert", None, "shard"),
        ),
        check_vma=False,
    )
```

profile of v0, /device:TPU:0, one launch (start us, length us, event | category | flops | bytes accessed | tf_op | source)
XLA Modules:
  0.0 71.5 jit_solution(4790408322568186875)
XLA Ops:
  0.6 1.4 %copy.11.expert_ids = s32[24,2]{1,0:T(8,128)} copy(s32[24,2]{0,1:T(2,128)} %param.8) | data formatting | bytes 384 | tf_op args[1]
  2.0 54.8 %shard_map.94 = (bf16[64,4096]{1,0:T(8,128)(2,1)}, bf16[512,4096]{1,0:T(8,128)(2,1)}, bf16[512,1024]{1,0:T(8,128)(2,1)}, bf16[512,1024]{1,0:T(8,128)(2,1)}) custom-call(bf16[24,4096]{1,0:T(8,128)(2,1)} %tokens.1, s32[24,2]{1,0:T(8,128)} %copy.11.expert_ids, bf16[1,4096,1024]{2,1,0:T(8,128)(2,1)} %weight_gate.1, bf16[1,4096,1024]{2,1,0:T(8,128)(2,1)} %weight_up.1, ...), custom_call_target="tpu_custom_call" | custom-call | tf_op jit(solution)/shard_map/pallas_call | solution.py:418
  56.8 14.7 %shard_map.95 = (bf16[24,4096]{1,0:T(8,128)(2,1)}, f32[1,4096,1024]{2,1,0:T(8,128)}, f32[1,4096,1024]{2,1,0:T(8,128)}) custom-call(s32[24,2]{1,0:T(8,128)} %copy.11.expert_ids, bf16[64,4096]{1,0:T(8,128)(2,1)} %get-tuple-element.7.returned, bf16[512,4096]{1,0:T(8,128)(2,1)} %get-tuple-element.8.block_rows, bf16[512,1024]{1,0:T(8,128)(2,1)} %get-tuple-element.9.gate_rows, ...), custom_call_target="tpu_custom_call" | custom-call | tf_op jit(solution)/shard_map/pallas_call | solution.py:456
where the time goes:
time: 71.7 us; the launch traced here: 71.5 us
  Pallas kernels  69.5 us (97%)
  local copies, waits for them, and re-layouts  1.35 us (2%)
    pallas_call x1, Pallas kernels, on_device(): pl.pallas_call(functools.partial(exchange_kernel, groups, capacity, chunk...  54.8 us
    pallas_call x1, Pallas kernels, on_device(): pl.pallas_call(functools.partial(weight_grad_kernel, groups, capacity), g...  14.7 us

commit v1 on v0

v1 whole, which is shorter than its diff:
```python
import functools
import jax
import jax.numpy as jnp
from jax import lax
from jax.experimental import pallas as pl
from jax.experimental.pallas import tpu as pltpu
from jax.sharding import PartitionSpec as P

MESH = pl.DeviceIdType.MESH
GATHERS = 4
SUMS = 8
AHEAD = 3
STEPS = 17
ORDER = (
    ("multiply", 0, 1), ("pair_sum", 1, 1), ("near_sum", 4, 1), ("spread", 5, 2), ("own_sum", 6, 1),
    ("forward", 7, 2), ("far", 9, 2), ("gathered", 10, 2),
)


def swiglu_grads(gate_values, up_values, hidden_cotangent):
    gate_float = gate_values.astype(jnp.float32)
    up_float = up_values.astype(jnp.float32)
    cotangent = hidden_cotangent.astype(jnp.float32)
    sigmoid_gate = jax.nn.sigmoid(gate_float)
    gate_grad = (
        cotangent * up_float * sigmoid_gate * (1.0 + gate_float * (1.0 - sigmoid_gate))
    ).astype(jnp.bfloat16)
    up_grad = (cotangent * gate_float * sigmoid_gate).astype(jnp.bfloat16)
    return (gate_grad, up_grad)


def slot_table(expert_ids, groups, capacity):
    token_count = expert_ids.shape[0]
    choices_per = expert_ids.shape[1]
    labels = lax.broadcasted_iota(jnp.int32, (1, 1, groups), 2)
    one_hot = (expert_ids[:, :, None] == labels).astype(jnp.int32)
    flat_hits = one_hot.reshape(token_count * choices_per, groups)
    earlier = jnp.cumsum(flat_hits, axis=0) - flat_hits
    slot_index = jnp.sum(flat_hits * earlier, axis=1).reshape(token_count, choices_per)
    slot_labels = lax.broadcasted_iota(jnp.int32, (1, 1, 1, capacity), 3)
    slot_hits = one_hot[:, :, :, None] * (slot_index[:, :, None, None] == slot_labels).astype(
        jnp.int32
    )
    selection = jnp.sum(slot_hits, axis=1).reshape(token_count, groups * capacity)
    return selection.astype(jnp.bfloat16)


def rows_inner(left_rows, right_rows):
    return lax.dot_general(
        left_rows, right_rows, (((0,), (0,)), ((), ())), preferred_element_type=jnp.float32
    )


def times_transposed(left_rows, weights):
    return lax.dot_general(
        left_rows, weights, (((1,), (1,)), ((), ())), preferred_element_type=jnp.float32
    )


def on_device_general(tokens, expert_ids, weight_gate, weight_up, gate_pre, up_pre, hidden_grad):
    groups = lax.axis_size("expert")
    shards = lax.axis_size("shard")
    model_width = tokens.shape[1]
    capacity = gate_pre.shape[1] // (groups * shards)
    selection = slot_table(expert_ids, groups, capacity)
    outgoing = rows_inner(selection, tokens).astype(jnp.bfloat16)
    gate_grad, up_grad = swiglu_grads(gate_pre[0], up_pre[0], hidden_grad[0])
    gate_matrix = weight_gate[0]
    up_matrix = weight_up[0]
    arrived = lax.all_to_all(
        outgoing.reshape(groups, capacity, model_width),
        "expert",
        split_axis=0,
        concat_axis=0,
        tiled=True,
    )
    block_rows = lax.all_gather(
        arrived.reshape(groups * capacity, model_width), "shard", axis=0, tiled=True
    )
    gate_rows = gate_grad
    up_rows = up_grad
    gate_wgrad = rows_inner(block_rows, gate_rows)
    up_wgrad = rows_inner(block_rows, up_rows)
    gate_rows = gate_grad
    up_rows = up_grad
    summed = lax.psum_scatter(
        (times_transposed(gate_rows, gate_matrix) + times_transposed(up_rows, up_matrix)).astype(
            jnp.bfloat16
        ),
        "shard",
        scatter_dimension=0,
        tiled=True,
    )
    outbound = summed.reshape(groups, capacity, model_width)
    returned = lax.all_to_all(outbound, "expert", split_axis=0, concat_axis=0, tiled=True)
    returned = returned.reshape(groups * capacity, model_width)
    token_grad = times_transposed(selection, returned.T).astype(jnp.bfloat16)
    return (token_grad, gate_wgrad[None], up_wgrad[None])


def slot_choice(expert_ids, groups, capacity):
    token_count = expert_ids.shape[1]
    lines = lax.broadcasted_iota(jnp.int32, (groups * capacity, token_count), 0)
    expert, slot = lines // capacity, lines % capacity
    named = jnp.logical_or(expert_ids[0:1, :] == expert, expert_ids[1:2, :] == expert)
    hits = jnp.where(named, 1.0, 0.0)
    above = lax.broadcasted_iota(jnp.int32, (token_count, token_count), 0)
    below = lax.broadcasted_iota(jnp.int32, (token_count, token_count), 1)
    before = jnp.where(above < below, 1.0, 0.0)
    earlier = jnp.dot(hits, before, preferred_element_type=jnp.float32)
    chosen = jnp.logical_and(named, earlier == slot.astype(jnp.float32))
    return jnp.where(chosen, 1.0, 0.0).astype(jnp.bfloat16)


def exchange_kernel(
    groups, capacity, expert_ids, tokens, weight_gate, weight_up, gate_pre, up_pre, hidden_grad,
    returned_out, block_rows, gate_out, up_out,
    token_buf, outgoing, weights, pre, gate_rows, up_rows, block, partial, from_core, total, from_diag,
    from_near, leaving, returned, load_sem, store_sem, send_sem, gather_sem, sum_sem, return_sem,
):
    e = lax.axis_index("expert")
    q = lax.axis_index("shard")
    core, x, y = q % 2, (q // 2) % 2, q // 4
    sib = q + 1 - 2 * core
    xn = q + 2 - 4 * x
    yn = q + 4 - 8 * y
    dg = xn + 4 - 8 * y
    rows = groups * capacity
    half = rows // 2
    slots = gate_rows.shape[0]
    wide = block.shape[2]
    slim = total.shape[2]

    def columns(c, width):
        return pl.ds(pl.multiple_of(c * width, width), width)

    def span(start, size):
        return pl.ds(pl.multiple_of(start, size), size)

    def held(c, start, size):
        return block.at[c, span(start, size), :]

    def chip_rows(c, device, low, size):
        return total.at[c, span(device // 2 * rows + low, size), :]

    def other(k):
        return (e + k) % groups

    def wait(place, sem):
        pltpu.make_async_copy(place, place, sem).wait()

    def target(k):
        if k < 3:
            return (other(k + 1), q)
        if k >= 18:
            return (other(k - 17), q)
        if k in (3, 7, 12, 14, 16):
            return (e, xn)
        if k in (4, 6, 13, 15, 17):
            return (e, yn)
        return (e, sib)

    def copy(k, c):
        if k < 3:
            source = outgoing.at[other(k + 1), :, columns(c, wide)]
            to = held(c, q * rows + e * capacity, capacity)
        elif k < 6:
            source = to = held(c, q * rows, rows)
        elif k == 6:
            source = to = held(c, xn * rows, half)
        elif k == 7:
            source = to = held(c, yn * rows + half, half)
        elif k < 11:
            source = to = held(c, (xn, yn, dg)[k - 8] * rows, rows)
        elif k == 11:
            source, to = partial.at[c, 1 - core], from_core.at[c]
        elif k == 12:
            source, to = chip_rows(c, dg, 0, half), from_diag.at[c, 0]
        elif k == 13:
            source, to = chip_rows(c, dg, half, half), from_diag.at[c, 1]
        elif k == 14:
            source, to = chip_rows(c, xn, 0, half), from_near.at[c, 0, 0]
        elif k == 15:
            source, to = chip_rows(c, yn, half, half), from_near.at[c, 1, 1]
        elif k == 16:
            source, to = chip_rows(c, xn, half, half), from_near.at[c, 0, 1]
        elif k == 17:
            source, to = chip_rows(c, yn, 0, half), from_near.at[c, 1, 0]
        else:
            source = leaving.at[c, span(other(k - 17) * capacity, capacity), :]
            to = returned.at[c, span(e * capacity, capacity), :]
        if k < 11:
            recv = gather_sem.at[c, (0, 0, 0, 1, 2, 4, 3, 3, 4, 4, 4)[k]]
        elif k < 18:
            recv = sum_sem.at[c, (0, 1, 1, 2, 2, 2, 2)[k - 11]]
        else:
            recv = return_sem.at[0]
        return pltpu.make_async_remote_copy(
            src_ref=source, dst_ref=to, send_sem=send_sem.at[0], recv_sem=recv,
            device_id=target(k), device_id_type=MESH,
        )

    def weight_loads(c):
        for i, source in enumerate((weight_gate, weight_up)):
            pltpu.make_async_copy(
                source.at[0, columns(c, slim), :], weights.at[c, i], load_sem.at[c]
            ).start()

    token_load = pltpu.make_async_copy(tokens, token_buf, load_sem.at[SUMS])
    token_load.start()
    for i, source in enumerate((gate_pre, up_pre, hidden_grad)):
        pltpu.make_async_copy(source.at[0], pre.at[i], load_sem.at[SUMS + 1]).start()
    for c in range(AHEAD):
        weight_loads(c)

    barrier = pltpu.get_barrier_semaphore()
    for device in ((other(1), q), (other(2), q), (other(3), q), (e, sib), (e, xn), (e, yn)):
        pl.semaphore_signal(barrier, inc=1, device_id=device, device_id_type=MESH)
    selection = slot_choice(expert_ids[...], groups, capacity)
    token_load.wait()
    for c in range(GATHERS):
        here = slice(c * wide, (c + 1) * wide)
        picked = jnp.dot(
            selection, token_buf[:, here], preferred_element_type=jnp.float32
        ).astype(jnp.bfloat16)
        for group in range(groups):
            outgoing[group, :, here] = picked[group * capacity : (group + 1) * capacity]

    @pl.loop(0, GATHERS)
    def _(c):
        block[c, span(q * rows + e * capacity, capacity), :] = outgoing[e, :, columns(c, wide)]

    wait(pre, load_sem.at[SUMS + 1])
    step_rows = 32

    @pl.loop(0, slots // step_rows)
    def _(i):
        here = span(i * step_rows, step_rows)
        gate_grad, up_grad = swiglu_grads(pre[0, here, :], pre[1, here, :], pre[2, here, :])
        gate_rows[here, :] = gate_grad
        up_rows[here, :] = up_grad

    for i in range(2):
        pltpu.make_async_copy(
            (gate_rows, up_rows)[i], (gate_out, up_out)[i], store_sem.at[0, i]
        ).start()

    def multiply(c):
        @pl.when(c < SUMS - AHEAD)
        def _():
            weight_loads(c + AHEAD)

        wait(weights.at[c], load_sem.at[c])
        term = times_transposed(gate_rows[...], weights[c, 0]) + times_transposed(
            up_rows[...], weights[c, 1]
        )
        term = term.astype(jnp.bfloat16)
        for chip in range(slots // (2 * rows)):
            for side in range(2):
                low = (2 * chip + side) * rows
                partial[c, side, chip * rows : (chip + 1) * rows, :] = term[low : low + rows]

        @pl.when(c == 0)
        def _():
            pl.semaphore_wait(barrier, 6)

            @pl.loop(0, GATHERS)
            def _(i):
                for k in (1, 0, 2):
                    copy(k, i).start()

        copy(11, c).start()

    def spread(c):
        wait(held(c, 0, 3 * capacity), gather_sem.at[c, 0])
        for k in (3, 4, 5):
            copy(k, c).start()

    def forward(c):
        wait(held(c, 0, rows), gather_sem.at[c, 1])
        copy(6, c).start()
        copy(8, c).start()
        wait(held(c, 0, rows), gather_sem.at[c, 2])
        copy(7, c).start()
        copy(9, c).start()

    def far(c):
        wait(held(c, 0, rows), gather_sem.at[c, 3])
        copy(10, c).start()

    def gathered(c):
        wait(held(c, 0, 4 * rows), gather_sem.at[c, 4])
        pltpu.make_async_copy(
            block.at[c], block_rows.at[:, columns(c, wide)], store_sem.at[1, c]
        ).start()

    def pair_sum(c):
        wait(from_core.at[c], sum_sem.at[c, 0])
        both = partial[c, core].astype(jnp.float32) + from_core[c].astype(jnp.float32)
        total[c] = both.astype(jnp.bfloat16)
        for k in (12, 13, 14, 15):
            copy(k, c).start()

    def near_sum(c):
        wait(from_diag.at[c], sum_sem.at[c, 1])
        for side, device, low in ((0, yn, 0), (1, xn, half)):
            place = span(device // 2 * rows + low, half)
            added = total[c, place, :].astype(jnp.float32) + from_diag[c, side].astype(jnp.float32)
            total[c, place, :] = added.astype(jnp.bfloat16)
            copy(17 if side == 0 else 16, c).start()

    def own_sum(c):
        wait(from_near.at[c], sum_sem.at[c, 2])
        for low in range(2):
            place = span(q // 2 * rows + low * half, half)
            added = total[c, place, :].astype(jnp.float32)
            added = added + from_near[c, 0, low].astype(jnp.float32)
            added = added + from_near[c, 1, low].astype(jnp.float32)
            leaving[c, low * half : (low + 1) * half, :] = added.astype(jnp.bfloat16)
        mine = span(e * capacity, capacity)
        returned[c, mine, :] = leaving[c, mine, :]
        for k in (19, 18, 20):
            copy(k, c).start()

    @pl.loop(0, STEPS)
    def _(step):
        for name, first, every in ORDER:
            stage = dict(
                multiply=multiply, pair_sum=pair_sum, near_sum=near_sum, own_sum=own_sum,
                spread=spread, forward=forward, far=far, gathered=gathered,
            )[name]
            count = GATHERS if name in ("spread", "forward", "far", "gathered") else SUMS
            c = (step - first) // every
            ready = jnp.logical_and(step >= first, step < first + every * count)
            if every > 1:
                ready = jnp.logical_and(ready, (step - first) % every == 0)

            @pl.when(ready)
            def _():
                stage(c)

    wait(returned.at[:, pl.ds(0, 3 * capacity), :], return_sem.at[0])
    for c in range(SUMS):
        pltpu.make_async_copy(
            returned.at[c], returned_out.at[:, columns(c, slim)], store_sem.at[2, 0]
        ).start()
    sent = (6 * capacity + 6 * rows + 8 * half + slots // 2) * SUMS * slim // weight_gate.shape[2]
    wait(weight_gate.at[0, pl.ds(0, sent), :], send_sem.at[0])
    for c in range(GATHERS):
        wait(block.at[c], store_sem.at[1, c])
    wait(returned, store_sem.at[2, 0])
    wait(gate_rows, store_sem.at[0, 0])
    wait(up_rows, store_sem.at[0, 1])


def weight_grad_kernel(
    groups, capacity, expert_ids, returned, block_rows, gate_rows, up_rows,
    token_grad, gate_wgrad, up_wgrad, selection,
):
    @pl.when(pl.program_id(0) == 0)
    def _():
        selection[...] = slot_choice(expert_ids[...], groups, capacity)

    left = block_rows[...]
    gate_wgrad[0] = rows_inner(left, gate_rows[...])
    up_wgrad[0] = rows_inner(left, up_rows[...])
    token_grad[...] = rows_inner(selection[...], returned[...]).astype(jnp.bfloat16)


def on_device(tokens, expert_ids, weight_gate, weight_up, gate_pre, up_pre, hidden_grad):
    groups = lax.axis_size("expert")
    shards = lax.axis_size("shard")
    token_count, model_width = tokens.shape
    slots, hidden = gate_pre.shape[1:]
    capacity = slots // (groups * shards)
    rows = groups * capacity
    wide = model_width // GATHERS
    slim = model_width // SUMS
    bf16 = jnp.bfloat16
    choices = expert_ids.T
    in_vmem = pl.BlockSpec(memory_space=pltpu.VMEM)
    anywhere = pl.BlockSpec(memory_space=pl.ANY)
    returned, block_rows, gate_rows, up_rows = pl.pallas_call(
        functools.partial(exchange_kernel, groups, capacity),
        out_shape=(
            jax.ShapeDtypeStruct((rows, model_width), bf16),
            jax.ShapeDtypeStruct((slots, model_width), bf16),
            jax.ShapeDtypeStruct((slots, hidden), bf16),
            jax.ShapeDtypeStruct((slots, hidden), bf16),
        ),
        in_specs=[in_vmem] + [anywhere] * 6,
        out_specs=(anywhere, anywhere, anywhere, anywhere),
        scratch_shapes=[
            pltpu.VMEM((token_count, model_width), bf16),
            pltpu.VMEM((groups, capacity, model_width), bf16),
            pltpu.VMEM((SUMS, 2, slim, hidden), bf16),
            pltpu.VMEM((3, slots, hidden), bf16),
            pltpu.VMEM((slots, hidden), bf16),
            pltpu.VMEM((slots, hidden), bf16),
            pltpu.VMEM((GATHERS, slots, wide), bf16),
            pltpu.VMEM((SUMS, 2, slots // 2, slim), bf16),
            pltpu.VMEM((SUMS, slots // 2, slim), bf16),
            pltpu.VMEM((SUMS, slots // 2, slim), bf16),
            pltpu.VMEM((SUMS, 2, rows // 2, slim), bf16),
            pltpu.VMEM((SUMS, 2, 2, rows // 2, slim), bf16),
            pltpu.VMEM((SUMS, rows, slim), bf16),
            pltpu.VMEM((SUMS, rows, slim), bf16),
            pltpu.SemaphoreType.DMA((SUMS + 2,)),
            pltpu.SemaphoreType.DMA((3, GATHERS)),
            pltpu.SemaphoreType.DMA((1,)),
            pltpu.SemaphoreType.DMA((GATHERS, 5)),
            pltpu.SemaphoreType.DMA((SUMS, 3)),
            pltpu.SemaphoreType.DMA((1,)),
        ],
        compiler_params=pltpu.CompilerParams(
            collective_id=0, has_side_effects=True, vmem_limit_bytes=60 * 1024 * 1024
        ),
    )(choices, tokens, weight_gate, weight_up, gate_pre, up_pre, hidden_grad)
    tile = min(512, model_width)
    wgrad_shape = jax.ShapeDtypeStruct((1, model_width, hidden), jnp.float32)
    token_grad, gate_wgrad, up_wgrad = pl.pallas_call(
        functools.partial(weight_grad_kernel, groups, capacity),
        grid=(model_width // tile,),
        out_shape=(jax.ShapeDtypeStruct((token_count, model_width), bf16), wgrad_shape, wgrad_shape),
        in_specs=[
            pl.BlockSpec(choices.shape, lambda i: (0, 0)),
            pl.BlockSpec((rows, tile), lambda i: (0, i)),
            pl.BlockSpec((slots, tile), lambda i: (0, i)),
            pl.BlockSpec((slots, hidden), lambda i: (0, 0)),
            pl.BlockSpec((slots, hidden), lambda i: (0, 0)),
        ],
        out_specs=(
            pl.BlockSpec((token_count, tile), lambda i: (0, i)),
            pl.BlockSpec((1, tile, hidden), lambda i: (0, i, 0)),
            pl.BlockSpec((1, tile, hidden), lambda i: (0, i, 0)),
        ),
        scratch_shapes=[pltpu.VMEM((rows, token_count), bf16)],
        compiler_params=pltpu.CompilerParams(vmem_limit_bytes=63 * 1024 * 1024),
    )(choices, returned, block_rows, gate_rows, up_rows)
    return (token_grad, gate_wgrad, up_wgrad)


def solution(mesh):
    placed = (
        P(("expert", "shard"), None),
        P(("expert", "shard"), None),
        P("expert", None, "shard"),
        P("expert", None, "shard"),
        P("expert", None, "shard"),
        P("expert", None, "shard"),
        P("expert", None, "shard"),
    )
    small = mesh.shape["shard"] == 8 and mesh.shape["expert"] == 4
    return jax.shard_map(
        on_device if small else on_device_general,
        mesh=mesh,
        in_specs=placed,
        out_specs=(
            P(("expert", "shard"), None),
            P("expert", None, "shard"),
            P("expert", None, "shard"),
        ),
        check_vma=False,
    )
```

time: 71.7 us -> 64.1 us (0.89); the launches traced: 71.5 us -> 62.9 us
  Pallas kernels: 69.5 us -> 62.3 us
  local copies, waits for them, and re-layouts: 1.35 us -> 0 us
    pallas_call x1, Pallas kernels: 54.8 us -> 47.7 us  [on_device(): pl.pallas_call(functools.partial(exchange_kernel, groups, capacity), out_...]
    unnamed x1 -> x0, local copies, waits for them, and re-layouts: 1.35 us -> none
where the time goes in v1:
time: 64.1 us; the launch traced here: 62.9 us
  Pallas kernels  62.3 us (97%)
    pallas_call x1, Pallas kernels, on_device(): pl.pallas_call(functools.partial(exchange_kernel, groups, capacity), out_...  47.7 us
    pallas_call x1, Pallas kernels, on_device(): pl.pallas_call(functools.partial(weight_grad_kernel, groups, capacity), g...  14.5 us

profile of v1, /device:TPU:0, one launch (start us, length us, event | category | flops | bytes accessed | tf_op | source)
XLA Modules:
  0.0 62.9 jit_solution(16909270536481844791)
XLA Ops:
  0.6 47.7 %shard_map.94 = (bf16[64,4096]{1,0:T(8,128)(2,1)}, bf16[512,4096]{1,0:T(8,128)(2,1)}, bf16[512,1024]{1,0:T(8,128)(2,1)}, bf16[512,1024]{1,0:T(8,128)(2,1)}) custom-call(s32[2,24]{1,0:T(2,128)} %bitcast.1, bf16[24,4096]{1,0:T(8,128)(2,1)} %tokens.1, bf16[1,4096,1024]{2,1,0:T(8,128)(2,1)} %weight_gate.1, bf16[1,4096,1024]{2,1,0:T(8,128)(2,1)} %weight_up.1, ...), custom_call_target="tpu_custom_call" | custom-call | tf_op jit(solution)/shard_map/pallas_call | solution.py:383
  48.4 14.5 %shard_map.95 = (bf16[24,4096]{1,0:T(8,128)(2,1)}, f32[1,4096,1024]{2,1,0:T(8,128)}, f32[1,4096,1024]{2,1,0:T(8,128)}) custom-call(s32[2,24]{1,0:T(2,128)} %bitcast.2, bf16[64,4096]{1,0:T(8,128)(2,1)} %get-tuple-element.7.returned, bf16[512,4096]{1,0:T(8,128)(2,1)} %get-tuple-element.8.block_rows, bf16[512,1024]{1,0:T(8,128)(2,1)} %get-tuple-element.9.gate_rows, ...), custom_call_target="tpu_custom_call" | custom-call | tf_op jit(solution)/shard_map/pallas_call | solution.py:421

commit v2 on v1

--- a/solution.py
+++ b/solution.py
@@ -12,8 +12,14 @@
 AHEAD = 3
 STEPS = 17
 ORDER = (
-    ("multiply", 0, 1), ("pair_sum", 1, 1), ("near_sum", 4, 1), ("spread", 5, 2), ("own_sum", 6, 1),
-    ("forward", 7, 2), ("far", 9, 2), ("gathered", 10, 2),
+    ("multiply", 0, 1),
+    ("pair_sum", 1, 1),
+    ("near_sum", 4, 1),
+    ("spread", 5, 2),
+    ("own_sum", 6, 1),
+    ("forward", 7, 2),
+    ("far", 9, 2),
+    ("gathered", 10, 2),
 )
 
 
@@ -114,9 +120,9 @@
 
 def exchange_kernel(
     groups, capacity, expert_ids, tokens, weight_gate, weight_up, gate_pre, up_pre, hidden_grad,
-    returned_out, block_rows, gate_out, up_out,
-    token_buf, outgoing, weights, pre, gate_rows, up_rows, block, partial, from_core, total, from_diag,
-    from_near, leaving, returned, load_sem, store_sem, send_sem, gather_sem, sum_sem, return_sem,
+    returned, block, gate_rows, up_rows, selection,
+    choices, token_buf, outgoing, weights, pre, partial, from_core, total, from_diag,
+    from_near, leaving, load_sem, send_sem, gather_sem, sum_sem, return_sem,
 ):
     e = lax.axis_index("expert")
     q = lax.axis_index("shard")
@@ -128,7 +134,7 @@
     rows = groups * capacity
     half = rows // 2
     slots = gate_rows.shape[0]
-    wide = block.shape[2]
+    wide = block.shape[1] // GATHERS
     slim = total.shape[2]
 
     def columns(c, width):
@@ -138,7 +144,7 @@
         return pl.ds(pl.multiple_of(start, size), size)
 
     def held(c, start, size):
-        return block.at[c, span(start, size), :]
+        return block.at[span(start, size), columns(c, wide)]
 
     def chip_rows(c, device, low, size):
         return total.at[c, span(device // 2 * rows + low, size), :]
@@ -188,7 +194,7 @@
             source, to = chip_rows(c, yn, 0, half), from_near.at[c, 1, 0]
         else:
             source = leaving.at[c, span(other(k - 17) * capacity, capacity), :]
-            to = returned.at[c, span(e * capacity, capacity), :]
+            to = returned.at[span(e * capacity, capacity), columns(c, slim)]
         if k < 11:
             recv = gather_sem.at[c, (0, 0, 0, 1, 2, 4, 3, 3, 4, 4, 4)[k]]
         elif k < 18:
@@ -208,6 +214,8 @@
 
     token_load = pltpu.make_async_copy(tokens, token_buf, load_sem.at[SUMS])
     token_load.start()
+    choice_load = pltpu.make_async_copy(expert_ids, choices, load_sem.at[SUMS + 2])
+    choice_load.start()
     for i, source in enumerate((gate_pre, up_pre, hidden_grad)):
         pltpu.make_async_copy(source.at[0], pre.at[i], load_sem.at[SUMS + 1]).start()
     for c in range(AHEAD):
@@ -216,19 +224,21 @@
     barrier = pltpu.get_barrier_semaphore()
     for device in ((other(1), q), (other(2), q), (other(3), q), (e, sib), (e, xn), (e, yn)):
         pl.semaphore_signal(barrier, inc=1, device_id=device, device_id_type=MESH)
-    selection = slot_choice(expert_ids[...], groups, capacity)
+    choice_load.wait()
+    selection[...] = slot_choice(choices[...], groups, capacity)
     token_load.wait()
     for c in range(GATHERS):
         here = slice(c * wide, (c + 1) * wide)
         picked = jnp.dot(
-            selection, token_buf[:, here], preferred_element_type=jnp.float32
+            selection[...], token_buf[:, here], preferred_element_type=jnp.float32
         ).astype(jnp.bfloat16)
         for group in range(groups):
             outgoing[group, :, here] = picked[group * capacity : (group + 1) * capacity]
 
     @pl.loop(0, GATHERS)
     def _(c):
-        block[c, span(q * rows + e * capacity, capacity), :] = outgoing[e, :, columns(c, wide)]
+        here = columns(c, wide)
+        block[span(q * rows + e * capacity, capacity), here] = outgoing[e, :, here]
 
     wait(pre, load_sem.at[SUMS + 1])
     step_rows = 32
@@ -239,11 +249,6 @@
         gate_grad, up_grad = swiglu_grads(pre[0, here, :], pre[1, here, :], pre[2, here, :])
         gate_rows[here, :] = gate_grad
         up_rows[here, :] = up_grad
-
-    for i in range(2):
-        pltpu.make_async_copy(
-            (gate_rows, up_rows)[i], (gate_out, up_out)[i], store_sem.at[0, i]
-        ).start()
 
     def multiply(c):
         @pl.when(c < SUMS - AHEAD)
@@ -290,9 +295,6 @@
 
     def gathered(c):
         wait(held(c, 0, 4 * rows), gather_sem.at[c, 4])
-        pltpu.make_async_copy(
-            block.at[c], block_rows.at[:, columns(c, wide)], store_sem.at[1, c]
-        ).start()
 
     def pair_sum(c):
         wait(from_core.at[c], sum_sem.at[c, 0])
@@ -318,7 +320,7 @@
             added = added + from_near[c, 1, low].astype(jnp.float32)
             leaving[c, low * half : (low + 1) * half, :] = added.astype(jnp.bfloat16)
         mine = span(e * capacity, capacity)
-        returned[c, mine, :] = leaving[c, mine, :]
+        returned[mine, columns(c, slim)] = leaving[c, mine, :]
         for k in (19, 18, 20):
             copy(k, c).start()
 
@@ -339,32 +341,20 @@
             def _():
                 stage(c)
 
-    wait(returned.at[:, pl.ds(0, 3 * capacity), :], return_sem.at[0])
-    for c in range(SUMS):
-        pltpu.make_async_copy(
-            returned.at[c], returned_out.at[:, columns(c, slim)], store_sem.at[2, 0]
-        ).start()
+    wait(returned.at[pl.ds(0, 3 * capacity), :], return_sem.at[0])
     sent = (6 * capacity + 6 * rows + 8 * half + slots // 2) * SUMS * slim // weight_gate.shape[2]
     wait(weight_gate.at[0, pl.ds(0, sent), :], send_sem.at[0])
-    for c in range(GATHERS):
-        wait(block.at[c], store_sem.at[1, c])
-    wait(returned, store_sem.at[2, 0])
-    wait(gate_rows, store_sem.at[0, 0])
-    wait(up_rows, store_sem.at[0, 1])
 
 
 def weight_grad_kernel(
-    groups, capacity, expert_ids, returned, block_rows, gate_rows, up_rows,
-    token_grad, gate_wgrad, up_wgrad, selection,
+    returned, block_rows, gate_rows, up_rows, selection, token_grad, gate_wgrad, up_wgrad,
 ):
-    @pl.when(pl.program_id(0) == 0)
-    def _():
-        selection[...] = slot_choice(expert_ids[...], groups, capacity)
-
-    left = block_rows[...]
+    tile = gate_wgrad.shape[1]
+    here = pl.ds(pl.multiple_of(pl.program_id(0) * tile, tile), tile)
+    left = block_rows[:, here]
     gate_wgrad[0] = rows_inner(left, gate_rows[...])
     up_wgrad[0] = rows_inner(left, up_rows[...])
-    token_grad[...] = rows_inner(selection[...], returned[...]).astype(jnp.bfloat16)
+    token_grad[...] = rows_inner(selection[...], returned[:, here]).astype(jnp.bfloat16)
 
 
 def on_device(tokens, expert_ids, weight_gate, weight_up, gate_pre, up_pre, hidden_grad):
@@ -374,69 +364,61 @@
     slots, hidden = gate_pre.shape[1:]
     capacity = slots // (groups * shards)
     rows = groups * capacity
-    wide = model_width // GATHERS
     slim = model_width // SUMS
     bf16 = jnp.bfloat16
-    choices = expert_ids.T
+    kept = [
+        pltpu.with_memory_space_constraint(array, pltpu.HBM)
+        for array in (expert_ids.T, tokens, weight_gate, weight_up, gate_pre, up_pre, hidden_grad)
+    ]
     in_vmem = pl.BlockSpec(memory_space=pltpu.VMEM)
-    anywhere = pl.BlockSpec(memory_space=pl.ANY)
-    returned, block_rows, gate_rows, up_rows = pl.pallas_call(
+    in_hbm = pl.BlockSpec(memory_space=pltpu.HBM)
+    returned, block_rows, gate_rows, up_rows, selection = pl.pallas_call(
         functools.partial(exchange_kernel, groups, capacity),
         out_shape=(
             jax.ShapeDtypeStruct((rows, model_width), bf16),
             jax.ShapeDtypeStruct((slots, model_width), bf16),
             jax.ShapeDtypeStruct((slots, hidden), bf16),
             jax.ShapeDtypeStruct((slots, hidden), bf16),
+            jax.ShapeDtypeStruct((rows, token_count), bf16),
         ),
-        in_specs=[in_vmem] + [anywhere] * 6,
-        out_specs=(anywhere, anywhere, anywhere, anywhere),
+        in_specs=[in_hbm] * 7,
+        out_specs=(in_vmem,) * 5,
         scratch_shapes=[
+            pltpu.VMEM(expert_ids.shape[::-1], expert_ids.dtype),
             pltpu.VMEM((token_count, model_width), bf16),
             pltpu.VMEM((groups, capacity, model_width), bf16),
             pltpu.VMEM((SUMS, 2, slim, hidden), bf16),
             pltpu.VMEM((3, slots, hidden), bf16),
-            pltpu.VMEM((slots, hidden), bf16),
-            pltpu.VMEM((slots, hidden), bf16),
-            pltpu.VMEM((GATHERS, slots, wide), bf16),
             pltpu.VMEM((SUMS, 2, slots // 2, slim), bf16),
             pltpu.VMEM((SUMS, slots // 2, slim), bf16),
             pltpu.VMEM((SUMS, slots // 2, slim), bf16),
             pltpu.VMEM((SUMS, 2, rows // 2, slim), bf16),
             pltpu.VMEM((SUMS, 2, 2, rows // 2, slim), bf16),
             pltpu.VMEM((SUMS, rows, slim), bf16),
-            pltpu.VMEM((SUMS, rows, slim), bf16),
-            pltpu.SemaphoreType.DMA((SUMS + 2,)),
-            pltpu.SemaphoreType.DMA((3, GATHERS)),
+            pltpu.SemaphoreType.DMA((SUMS + 3,)),
             pltpu.SemaphoreType.DMA((1,)),
             pltpu.SemaphoreType.DMA((GATHERS, 5)),
             pltpu.SemaphoreType.DMA((SUMS, 3)),
             pltpu.SemaphoreType.DMA((1,)),
         ],
         compiler_params=pltpu.CompilerParams(
-            collective_id=0, has_side_effects=True, vmem_limit_bytes=60 * 1024 * 1024
+            collective_id=0, has_side_effects=True, vmem_limit_bytes=40 * 1024 * 1024
         ),
-    )(choices, tokens, weight_gate, weight_up, gate_pre, up_pre, hidden_grad)
+    )(*kept)
     tile = min(512, model_width)
     wgrad_shape = jax.ShapeDtypeStruct((1, model_width, hidden), jnp.float32)
     token_grad, gate_wgrad, up_wgrad = pl.pallas_call(
-        functools.partial(weight_grad_kernel, groups, capacity),
+        weight_grad_kernel,
         grid=(model_width // tile,),
         out_shape=(jax.ShapeDtypeStruct((token_count, model_width), bf16), wgrad_shape, wgrad_shape),
-        in_specs=[
-            pl.BlockSpec(choices.shape, lambda i: (0, 0)),
-            pl.BlockSpec((rows, tile), lambda i: (0, i)),
-            pl.BlockSpec((slots, tile), lambda i: (0, i)),
-            pl.BlockSpec((slots, hidden), lambda i: (0, 0)),
-            pl.BlockSpec((slots, hidden), lambda i: (0, 0)),
-        ],
+        in_specs=[in_vmem] * 5,
         out_specs=(
             pl.BlockSpec((token_count, tile), lambda i: (0, i)),
             pl.BlockSpec((1, tile, hidden), lambda i: (0, i, 0)),
             pl.BlockSpec((1, tile, hidden), lambda i: (0, i, 0)),
         ),
-        scratch_shapes=[pltpu.VMEM((rows, token_count), bf16)],
-        compiler_params=pltpu.CompilerParams(vmem_limit_bytes=63 * 1024 * 1024),
-    )(choices, returned, block_rows, gate_rows, up_rows)
+        compiler_params=pltpu.CompilerParams(vmem_limit_bytes=20 * 1024 * 1024),
+    )(returned, block_rows, gate_rows, up_rows, selection)
     return (token_grad, gate_wgrad, up_wgrad)
 
 

time: 64.1 us -> 59.8 us (0.933); the launches traced: 62.9 us -> 59.7 us
  Pallas kernels: 62.3 us -> 59 us
    pallas_call x1, Pallas kernels: 14.5 us -> 12.2 us  [on_device(): pl.pallas_call(weight_grad_kernel, grid=(model_width // tile,), out_shape...]
    pallas_call x1, Pallas kernels: 47.7 us -> 46.8 us  [on_device(): pl.pallas_call(functools.partial(exchange_kernel, groups, capacity), out_...]
where the time goes in v2:
time: 59.8 us; the launch traced here: 59.7 us
  Pallas kernels  59 us (99%)
  between operations  0.64 us (1%)
    pallas_call x1, Pallas kernels, on_device(): pl.pallas_call(functools.partial(exchange_kernel, groups, capacity), out_...  46.8 us
    pallas_call x1, Pallas kernels, on_device(): pl.pallas_call(weight_grad_kernel, grid=(model_width // tile,), out_shape...  12.2 us

profile of v2, /device:TPU:0, one launch (start us, length us, event | category | flops | bytes accessed | tf_op | source)
XLA Modules:
  0.0 59.7 jit_solution(13425480385042685245)
XLA Ops:
  0.6 46.8 %shard_map.94 = (bf16[64,4096]{1,0:T(8,128)(2,1)S(1)}, bf16[512,4096]{1,0:T(8,128)(2,1)S(1)}, bf16[512,1024]{1,0:T(8,128)(2,1)S(1)}, bf16[512,1024]{1,0:T(8,128)(2,1)S(1)}, bf16[64,24]{1,0:T(8,128)(2,1)S(1)}) custom-call(s32[2,24]{1,0:T(2,128)} %bitcast.1, bf16[24,4096]{1,0:T(8,128)(2,1)} %tokens.1, bf16[1,4096,1024]{2,1,0:T(8,128)(2,1)} %weight_gate.1, ...), custom_call_target="tpu_custom_call" | custom-call | tf_op jit(solution)/shard_map/pallas_call | solution.py:375
  47.5 12.2 %shard_map.95 = (bf16[24,4096]{1,0:T(8,128)(2,1)}, f32[1,4096,1024]{2,1,0:T(8,128)}, f32[1,4096,1024]{2,1,0:T(8,128)}) custom-call(bf16[64,4096]{1,0:T(8,128)(2,1)S(1)} %get-tuple-element.8.returned, bf16[512,4096]{1,0:T(8,128)(2,1)S(1)} %get-tuple-element.9.block_rows, bf16[512,1024]{1,0:T(8,128)(2,1)S(1)} %get-tuple-element.10.gate_rows, ...), custom_call_target="tpu_custom_call" | custom-call | tf_op jit(solution)/shard_map/pallas_call | solution.py:410

commit v3 on v2

--- a/solution.py
+++ b/solution.py
@@ -7,19 +7,23 @@
 from jax.sharding import PartitionSpec as P
 
 MESH = pl.DeviceIdType.MESH
-GATHERS = 4
+UNITS = 4
+GATHERS = 3
 SUMS = 8
 AHEAD = 3
-STEPS = 17
+STEPS = 20
 ORDER = (
     ("multiply", 0, 1),
     ("pair_sum", 1, 1),
-    ("near_sum", 4, 1),
-    ("spread", 5, 2),
-    ("own_sum", 6, 1),
-    ("forward", 7, 2),
-    ("far", 9, 2),
-    ("gathered", 10, 2),
+    ("token_spread", 4, 1),
+    ("near_sum", 3, 1),
+    ("own_sum", 5, 1),
+    ("spread", 7, 2),
+    ("forward", 9, 2),
+    ("token_pair", 12, 1),
+    ("far", 11, 2),
+    ("gathered", 13, 2),
+    ("token_end", 16, 1),
 )
 
 
@@ -121,8 +125,8 @@
 def exchange_kernel(
     groups, capacity, expert_ids, tokens, weight_gate, weight_up, gate_pre, up_pre, hidden_grad,
     returned, block, gate_rows, up_rows, selection,
-    choices, token_buf, outgoing, weights, pre, partial, from_core, total, from_diag,
-    from_near, leaving, load_sem, send_sem, gather_sem, sum_sem, return_sem,
+    choices, token_buf, outgoing, near_choices, near_tokens, near_outgoing, weights, pre, partial, from_core, total, from_diag,
+    from_near, leaving, load_sem, send_sem, gather_sem, token_sem, sum_sem, return_sem,
 ):
     e = lax.axis_index("expert")
     q = lax.axis_index("shard")
@@ -134,8 +138,11 @@
     rows = groups * capacity
     half = rows // 2
     slots = gate_rows.shape[0]
-    wide = block.shape[1] // GATHERS
+    wide = block.shape[1] // UNITS
     slim = total.shape[2]
+    tail = near_tokens.shape[2]
+    late = slice(GATHERS * wide, GATHERS * wide + tail)
+    peers = (q, xn, yn, dg)
 
     def columns(c, width):
         return pl.ds(pl.multiple_of(c * width, width), width)
@@ -206,6 +213,50 @@
             device_id=target(k), device_id_type=MESH,
         )
 
+    def remote(source, to, recv, device, sent):
+        return pltpu.make_async_remote_copy(
+            src_ref=source, dst_ref=to, send_sem=send_sem.at[sent], recv_sem=token_sem.at[recv],
+            device_id=device, device_id_type=MESH,
+        )
+
+    def announce():
+        for i, peer in enumerate(peers[1:]):
+            remote(choices, near_choices.at[i], 0, (e, peer), 1).start()
+            remote(token_buf.at[:, late], near_tokens.at[i], 1, (e, peer), 2).start()
+
+    def late_rows(peer, start, size):
+        return block.at[span(peer * rows + start, size), late]
+
+    def token_spread(c):
+        wait(near_choices, token_sem.at[0])
+        wait(near_tokens, token_sem.at[1])
+        for i in range(3):
+            picked = jnp.dot(
+                slot_choice(near_choices[i], groups, capacity), near_tokens[i],
+                preferred_element_type=jnp.float32,
+            ).astype(jnp.bfloat16)
+            for group in range(groups):
+                near_outgoing[i, group] = picked[group * capacity : (group + 1) * capacity]
+        for k in (1, 0, 2):
+            for i, peer in enumerate(peers):
+                if i == 0:
+                    source = outgoing.at[other(k + 1), :, late]
+                else:
+                    source = near_outgoing.at[i - 1, other(k + 1)]
+                to = late_rows(peer, e * capacity, capacity)
+                remote(source, to, 2, (other(k + 1), q), 3).start()
+        for i, peer in enumerate(peers[1:]):
+            block[span(peer * rows + e * capacity, capacity), late] = near_outgoing[i, e]
+
+    def token_pair(c):
+        wait(block.at[pl.ds(0, 12 * capacity), late], token_sem.at[2])
+        for peer in peers:
+            place = late_rows(peer, 0, rows)
+            remote(place, place, 3, (e, sib), 3).start()
+
+    def token_end(c):
+        wait(block.at[pl.ds(0, 4 * rows), late], token_sem.at[3])
+
     def weight_loads(c):
         for i, source in enumerate((weight_gate, weight_up)):
             pltpu.make_async_copy(
@@ -222,12 +273,12 @@
         weight_loads(c)
 
     barrier = pltpu.get_barrier_semaphore()
-    for device in ((other(1), q), (other(2), q), (other(3), q), (e, sib), (e, xn), (e, yn)):
+    for device in [(other(k), q) for k in (1, 2, 3)] + [(e, peer) for peer in (sib, xn, yn, dg)]:
         pl.semaphore_signal(barrier, inc=1, device_id=device, device_id_type=MESH)
     choice_load.wait()
     selection[...] = slot_choice(choices[...], groups, capacity)
     token_load.wait()
-    for c in range(GATHERS):
+    for c in range(UNITS):
         here = slice(c * wide, (c + 1) * wide)
         picked = jnp.dot(
             selection[...], token_buf[:, here], preferred_element_type=jnp.float32
@@ -235,7 +286,7 @@
         for group in range(groups):
             outgoing[group, :, here] = picked[group * capacity : (group + 1) * capacity]
 
-    @pl.loop(0, GATHERS)
+    @pl.loop(0, UNITS)
     def _(c):
         here = columns(c, wide)
         block[span(q * rows + e * capacity, capacity), here] = outgoing[e, :, here]
@@ -267,7 +318,8 @@
 
         @pl.when(c == 0)
         def _():
-            pl.semaphore_wait(barrier, 6)
+            pl.semaphore_wait(barrier, 7)
+            announce()
 
             @pl.loop(0, GATHERS)
             def _(i):
@@ -324,14 +376,17 @@
         for k in (19, 18, 20):
             copy(k, c).start()
 
+    stages = dict(
+        multiply=(multiply, SUMS), pair_sum=(pair_sum, SUMS), near_sum=(near_sum, SUMS),
+        own_sum=(own_sum, SUMS), spread=(spread, GATHERS), forward=(forward, GATHERS),
+        far=(far, GATHERS), gathered=(gathered, GATHERS), token_spread=(token_spread, 1),
+        token_pair=(token_pair, 1), token_end=(token_end, 1),
+    )
+
     @pl.loop(0, STEPS)
     def _(step):
         for name, first, every in ORDER:
-            stage = dict(
-                multiply=multiply, pair_sum=pair_sum, near_sum=near_sum, own_sum=own_sum,
-                spread=spread, forward=forward, far=far, gathered=gathered,
-            )[name]
-            count = GATHERS if name in ("spread", "forward", "far", "gathered") else SUMS
+            stage, count = stages[name]
             c = (step - first) // every
             ready = jnp.logical_and(step >= first, step < first + every * count)
             if every > 1:
@@ -342,8 +397,12 @@
                 stage(c)
 
     wait(returned.at[pl.ds(0, 3 * capacity), :], return_sem.at[0])
-    sent = (6 * capacity + 6 * rows + 8 * half + slots // 2) * SUMS * slim // weight_gate.shape[2]
-    wait(weight_gate.at[0, pl.ds(0, sent), :], send_sem.at[0])
+    sent = (3 * capacity + 6 * rows + 2 * half) * GATHERS * wide
+    sent = sent + (3 * capacity + 6 * half + slots // 2) * SUMS * slim
+    wait(weight_gate.at[0, pl.ds(0, sent // weight_gate.shape[2]), :], send_sem.at[0])
+    wait(near_choices, send_sem.at[1])
+    wait(near_tokens, send_sem.at[2])
+    wait(block.at[pl.ds(0, 12 * capacity + 4 * rows), late], send_sem.at[3])
 
 
 def weight_grad_kernel(
@@ -365,6 +424,7 @@
     capacity = slots // (groups * shards)
     rows = groups * capacity
     slim = model_width // SUMS
+    tail = model_width // UNITS * (UNITS - GATHERS)
     bf16 = jnp.bfloat16
     kept = [
         pltpu.with_memory_space_constraint(array, pltpu.HBM)
@@ -387,6 +447,9 @@
             pltpu.VMEM(expert_ids.shape[::-1], expert_ids.dtype),
             pltpu.VMEM((token_count, model_width), bf16),
             pltpu.VMEM((groups, capacity, model_width), bf16),
+            pltpu.VMEM((3, *expert_ids.shape[::-1]), expert_ids.dtype),
+            pltpu.VMEM((3, token_count, tail), bf16),
+            pltpu.VMEM((3, groups, capacity, tail), bf16),
             pltpu.VMEM((SUMS, 2, slim, hidden), bf16),
             pltpu.VMEM((3, slots, hidden), bf16),
             pltpu.VMEM((SUMS, 2, slots // 2, slim), bf16),
@@ -396,8 +459,9 @@
             pltpu.VMEM((SUMS, 2, 2, rows // 2, slim), bf16),
             pltpu.VMEM((SUMS, rows, slim), bf16),
             pltpu.SemaphoreType.DMA((SUMS + 3,)),
-            pltpu.SemaphoreType.DMA((1,)),
+            pltpu.SemaphoreType.DMA((4,)),
             pltpu.SemaphoreType.DMA((GATHERS, 5)),
+            pltpu.SemaphoreType.DMA((4,)),
             pltpu.SemaphoreType.DMA((SUMS, 3)),
             pltpu.SemaphoreType.DMA((1,)),
         ],

time: 59.8 us -> 55.6 us (0.930)
  Pallas kernels: 59 us -> 54.8 us
    pallas_call x1, Pallas kernels: 46.8 us -> 42.6 us  [on_device(): pl.pallas_call(functools.partial(exchange_kernel, groups, capacity), out_...]
where the time goes in v3:
time: 55.6 us; the launch traced here: 55.5 us
  Pallas kernels  54.8 us (99%)
  between operations  0.64 us (1%)
    pallas_call x1, Pallas kernels, on_device(): pl.pallas_call(functools.partial(exchange_kernel, groups, capacity), out_...  42.6 us
    pallas_call x1, Pallas kernels, on_device(): pl.pallas_call(weight_grad_kernel, grid=(model_width // tile,), out_shape...  12.2 us

profile of v3, /device:TPU:0, one launch (start us, length us, event | category | flops | bytes accessed | tf_op | source)
XLA Modules:
  0.0 55.5 jit_solution(7302692530110573641)
XLA Ops:
  0.6 42.6 %shard_map.94 = (bf16[64,4096]{1,0:T(8,128)(2,1)S(1)}, bf16[512,4096]{1,0:T(8,128)(2,1)S(1)}, bf16[512,1024]{1,0:T(8,128)(2,1)S(1)}, bf16[512,1024]{1,0:T(8,128)(2,1)S(1)}, bf16[64,24]{1,0:T(8,128)(2,1)S(1)}) custom-call(s32[2,24]{1,0:T(2,128)} %bitcast.1, bf16[24,4096]{1,0:T(8,128)(2,1)} %tokens.1, bf16[1,4096,1024]{2,1,0:T(8,128)(2,1)} %weight_gate.1, ...), custom_call_target="tpu_custom_call" | custom-call | tf_op jit(solution)/shard_map/pallas_call | solution.py:435
  43.3 12.2 %shard_map.95 = (bf16[24,4096]{1,0:T(8,128)(2,1)}, f32[1,4096,1024]{2,1,0:T(8,128)}, f32[1,4096,1024]{2,1,0:T(8,128)}) custom-call(bf16[64,4096]{1,0:T(8,128)(2,1)S(1)} %get-tuple-element.8.returned, bf16[512,4096]{1,0:T(8,128)(2,1)S(1)} %get-tuple-element.9.block_rows, bf16[512,1024]{1,0:T(8,128)(2,1)S(1)} %get-tuple-element.10.gate_rows, ...), custom_call_target="tpu_custom_call" | custom-call | tf_op jit(solution)/shard_map/pallas_call | solution.py:474

commit v4 on v3

--- a/solution.py
+++ b/solution.py
@@ -10,21 +10,25 @@
 UNITS = 4
 GATHERS = 3
 SUMS = 8
-AHEAD = 3
-STEPS = 20
+AHEAD = 2
+STEPS = 18
 ORDER = (
     ("multiply", 0, 1),
     ("pair_sum", 1, 1),
-    ("token_spread", 4, 1),
+    ("token_spread", 3, 1),
     ("near_sum", 3, 1),
     ("own_sum", 5, 1),
-    ("spread", 7, 2),
-    ("forward", 9, 2),
-    ("token_pair", 12, 1),
-    ("far", 11, 2),
-    ("gathered", 13, 2),
+    ("spread", 8, 1),
+    ("forward", 10, 1),
+    ("token_pair", 13, 1),
+    ("far", 12, 1),
+    ("gathered", 14, 1),
     ("token_end", 16, 1),
 )
+
+
+def tiles_of(quarter):
+    return (quarter // 2, quarter, quarter, quarter, quarter // 2)
 
 
 def swiglu_grads(gate_values, up_values, hidden_cotangent):
@@ -173,12 +177,14 @@
             return (e, yn)
         return (e, sib)
 
-    def copy(k, c):
+    def copy(k, c, piece=None):
         if k < 3:
             source = outgoing.at[other(k + 1), :, columns(c, wide)]
             to = held(c, q * rows + e * capacity, capacity)
         elif k < 6:
             source = to = held(c, q * rows, rows)
+            if piece is not None:
+                source = to = held(c, q * rows + other(piece) * capacity, capacity)
         elif k == 6:
             source = to = held(c, xn * rows, half)
         elif k == 7:
@@ -301,37 +307,31 @@
         gate_rows[here, :] = gate_grad
         up_rows[here, :] = up_grad
 
+    def products(c, low, size):
+        term = times_transposed(gate_rows[low : low + size, :], weights[c, 0])
+        term = term + times_transposed(up_rows[low : low + size, :], weights[c, 1])
+        term = term.astype(jnp.bfloat16)
+        for piece in range(size // rows):
+            chip, side = divmod(low // rows + piece, 2)
+            partial[c, side, chip * rows : (chip + 1) * rows, :] = term[
+                piece * rows : (piece + 1) * rows
+            ]
+
     def multiply(c):
         @pl.when(c < SUMS - AHEAD)
         def _():
             weight_loads(c + AHEAD)
 
         wait(weights.at[c], load_sem.at[c])
-        term = times_transposed(gate_rows[...], weights[c, 0]) + times_transposed(
-            up_rows[...], weights[c, 1]
-        )
-        term = term.astype(jnp.bfloat16)
-        for chip in range(slots // (2 * rows)):
-            for side in range(2):
-                low = (2 * chip + side) * rows
-                partial[c, side, chip * rows : (chip + 1) * rows, :] = term[low : low + rows]
-
-        @pl.when(c == 0)
-        def _():
-            pl.semaphore_wait(barrier, 7)
-            announce()
-
-            @pl.loop(0, GATHERS)
-            def _(i):
-                for k in (1, 0, 2):
-                    copy(k, i).start()
-
+        products(c, 0, slots)
         copy(11, c).start()
 
     def spread(c):
         wait(held(c, 0, 3 * capacity), gather_sem.at[c, 0])
-        for k in (3, 4, 5):
-            copy(k, c).start()
+        for k in (3, 4):
+            for piece in (1, 2, 3):
+                copy(k, c, piece).start()
+        copy(5, c).start()
 
     def forward(c):
         wait(held(c, 0, rows), gather_sem.at[c, 1])
@@ -376,6 +376,21 @@
         for k in (19, 18, 20):
             copy(k, c).start()
 
+    weight_loads(AHEAD)
+    wait(weights.at[0], load_sem.at[0])
+    products(0, 0, slots // 2)
+    pl.semaphore_wait(barrier, 7)
+    announce()
+
+    @pl.loop(0, GATHERS)
+    def _(c):
+        for k in (1, 0, 2):
+            copy(k, c).start()
+        for k in (3, 4):
+            copy(k, c, 0).start()
+
+    products(0, slots // 2, slots // 2)
+    copy(11, 0).start()
     stages = dict(
         multiply=(multiply, SUMS), pair_sum=(pair_sum, SUMS), near_sum=(near_sum, SUMS),
         own_sum=(own_sum, SUMS), spread=(spread, GATHERS), forward=(forward, GATHERS),
@@ -383,7 +398,7 @@
         token_pair=(token_pair, 1), token_end=(token_end, 1),
     )
 
-    @pl.loop(0, STEPS)
+    @pl.loop(1, STEPS)
     def _(step):
         for name, first, every in ORDER:
             stage, count = stages[name]
@@ -407,13 +422,31 @@
 
 def weight_grad_kernel(
     returned, block_rows, gate_rows, up_rows, selection, token_grad, gate_wgrad, up_wgrad,
+    staged, token_staged, store_sem, token_sem,
 ):
-    tile = gate_wgrad.shape[1]
-    here = pl.ds(pl.multiple_of(pl.program_id(0) * tile, tile), tile)
-    left = block_rows[:, here]
-    gate_wgrad[0] = rows_inner(left, gate_rows[...])
-    up_wgrad[0] = rows_inner(left, up_rows[...])
-    token_grad[...] = rows_inner(selection[...], returned[:, here]).astype(jnp.bfloat16)
+    quarter = block_rows.shape[1] // 4
+    tiles = tiles_of(quarter)
+    stores = []
+    low = 0
+    for i, tile in enumerate(tiles):
+        here = slice(low, low + tile)
+        for j, (grads, wgrad) in enumerate(((gate_rows, gate_wgrad), (up_rows, up_wgrad))):
+            if i >= 2:
+                stores[2 * i + j - 4].wait()
+            place = staged.at[i % 2, j, pl.ds(0, tile), :]
+            place[...] = rows_inner(block_rows[:, here], grads[...])
+            stores.append(
+                pltpu.make_async_copy(place, wgrad.at[0, pl.ds(low, tile), :], store_sem.at[i % 2, j])
+            )
+            stores[-1].start()
+        if i == 1:
+            token_staged[...] = rows_inner(selection[...], returned[...]).astype(jnp.bfloat16)
+            token_store = pltpu.make_async_copy(token_staged, token_grad, token_sem.at[0])
+            token_store.start()
+        low += tile
+    for store in stores[-4:]:
+        store.wait()
+    token_store.wait()
 
 
 def on_device(tokens, expert_ids, weight_gate, weight_up, gate_pre, up_pre, hidden_grad):
@@ -469,19 +502,19 @@
             collective_id=0, has_side_effects=True, vmem_limit_bytes=40 * 1024 * 1024
         ),
     )(*kept)
-    tile = min(512, model_width)
     wgrad_shape = jax.ShapeDtypeStruct((1, model_width, hidden), jnp.float32)
     token_grad, gate_wgrad, up_wgrad = pl.pallas_call(
         weight_grad_kernel,
-        grid=(model_width // tile,),
         out_shape=(jax.ShapeDtypeStruct((token_count, model_width), bf16), wgrad_shape, wgrad_shape),
         in_specs=[in_vmem] * 5,
-        out_specs=(
-            pl.BlockSpec((token_count, tile), lambda i: (0, i)),
-            pl.BlockSpec((1, tile, hidden), lambda i: (0, i, 0)),
-            pl.BlockSpec((1, tile, hidden), lambda i: (0, i, 0)),
-        ),
-        compiler_params=pltpu.CompilerParams(vmem_limit_bytes=20 * 1024 * 1024),
+        out_specs=(in_hbm,) * 3,
+        scratch_shapes=[
+            pltpu.VMEM((2, 2, model_width // 4, hidden), jnp.float32),
+            pltpu.VMEM((token_count, model_width), bf16),
+            pltpu.SemaphoreType.DMA((2, 2)),
+            pltpu.SemaphoreType.DMA((1,)),
+        ],
+        compiler_params=pltpu.CompilerParams(vmem_limit_bytes=26 * 1024 * 1024),
     )(returned, block_rows, gate_rows, up_rows, selection)
     return (token_grad, gate_wgrad, up_wgrad)
 

time: 55.6 us -> 53.9 us (0.969)
  Pallas kernels: 54.8 us -> 53.1 us
    pallas_call x1, Pallas kernels: 42.6 us -> 41.1 us  [on_device(): pl.pallas_call(functools.partial(exchange_kernel, groups, capacity), out_...]
where the time goes in v4:
time: 53.9 us; the launch traced here: 53.7 us
  Pallas kernels  53.1 us (99%)
  between operations  0.64 us (1%)
    pallas_call x1, Pallas kernels, on_device(): pl.pallas_call(functools.partial(exchange_kernel, groups, capacity), out_...  41.1 us
    pallas_call x1, Pallas kernels, on_device(): pl.pallas_call(weight_grad_kernel, out_shape=(jax.ShapeDtypeStruct((token...  12 us

profile of v4, /device:TPU:0, one launch (start us, length us, event | category | flops | bytes accessed | tf_op | source)
XLA Modules:
  0.0 53.7 jit_solution(8604331793464911356)
XLA Ops:
  0.6 41.1 %shard_map.94 = (bf16[64,4096]{1,0:T(8,128)(2,1)S(1)}, bf16[512,4096]{1,0:T(8,128)(2,1)S(1)}, bf16[512,1024]{1,0:T(8,128)(2,1)S(1)}, bf16[512,1024]{1,0:T(8,128)(2,1)S(1)}, bf16[64,24]{1,0:T(8,128)(2,1)S(1)}) custom-call(s32[2,24]{1,0:T(2,128)} %bitcast.1, bf16[24,4096]{1,0:T(8,128)(2,1)} %tokens.1, bf16[1,4096,1024]{2,1,0:T(8,128)(2,1)} %weight_gate.1, ...), custom_call_target="tpu_custom_call" | custom-call | tf_op jit(solution)/shard_map/pallas_call | solution.py:468
  41.7 12.0 %shard_map.95 = (bf16[24,4096]{1,0:T(8,128)(2,1)}, f32[1,4096,1024]{2,1,0:T(8,128)}, f32[1,4096,1024]{2,1,0:T(8,128)}) custom-call(bf16[64,4096]{1,0:T(8,128)(2,1)S(1)} %get-tuple-element.8.returned, bf16[512,4096]{1,0:T(8,128)(2,1)S(1)} %get-tuple-element.9.block_rows, bf16[512,1024]{1,0:T(8,128)(2,1)S(1)} %get-tuple-element.10.gate_rows, ...), custom_call_target="tpu_custom_call" | custom-call | tf_op jit(solution)/shard_map/pallas_call | solution.py:506

commit v5 on v4

--- a/solution.py
+++ b/solution.py
@@ -11,18 +11,19 @@
 GATHERS = 3
 SUMS = 8
 AHEAD = 2
-STEPS = 18
+STEPS = 19
 ORDER = (
     ("multiply", 0, 1),
+    ("token_forward", 2, 1),
     ("pair_sum", 1, 1),
-    ("token_spread", 3, 1),
     ("near_sum", 3, 1),
+    ("token_spread", 4, 1),
     ("own_sum", 5, 1),
-    ("spread", 8, 1),
-    ("forward", 10, 1),
-    ("token_pair", 13, 1),
-    ("far", 12, 1),
-    ("gathered", 14, 1),
+    ("spread", 9, 1),
+    ("forward", 11, 1),
+    ("token_pair", 14, 1),
+    ("far", 14, 1),
+    ("gathered", 16, 1),
     ("token_end", 16, 1),
 )
 
@@ -228,14 +229,23 @@
     def announce():
         for i, peer in enumerate(peers[1:]):
             remote(choices, near_choices.at[i], 0, (e, peer), 1).start()
-            remote(token_buf.at[:, late], near_tokens.at[i], 1, (e, peer), 2).start()
+        for i, peer in enumerate((xn, yn)):
+            remote(token_buf.at[:, late], near_tokens.at[i], 4 + i, (e, peer), 2).start()
+
+    def token_forward(c):
+        for i, peer in enumerate((yn, xn)):
+            wait(near_tokens.at[i], token_sem.at[4 + i])
+            here = slice(i * tail // 2, (i + 1) * tail // 2)
+            remote(
+                near_tokens.at[i, :, here], near_tokens.at[2, :, here], 1, (e, peer), 2
+            ).start()
 
     def late_rows(peer, start, size):
         return block.at[span(peer * rows + start, size), late]
 
     def token_spread(c):
         wait(near_choices, token_sem.at[0])
-        wait(near_tokens, token_sem.at[1])
+        wait(near_tokens.at[2], token_sem.at[1])
         for i in range(3):
             picked = jnp.dot(
                 slot_choice(near_choices[i], groups, capacity), near_tokens[i],
@@ -395,7 +405,7 @@
         multiply=(multiply, SUMS), pair_sum=(pair_sum, SUMS), near_sum=(near_sum, SUMS),
         own_sum=(own_sum, SUMS), spread=(spread, GATHERS), forward=(forward, GATHERS),
         far=(far, GATHERS), gathered=(gathered, GATHERS), token_spread=(token_spread, 1),
-        token_pair=(token_pair, 1), token_end=(token_end, 1),
+        token_forward=(token_forward, 1), token_pair=(token_pair, 1), token_end=(token_end, 1),
     )
 
     @pl.loop(1, STEPS)
@@ -494,7 +504,7 @@
             pltpu.SemaphoreType.DMA((SUMS + 3,)),
             pltpu.SemaphoreType.DMA((4,)),
             pltpu.SemaphoreType.DMA((GATHERS, 5)),
-            pltpu.SemaphoreType.DMA((4,)),
+            pltpu.SemaphoreType.DMA((6,)),
             pltpu.SemaphoreType.DMA((SUMS, 3)),
             pltpu.SemaphoreType.DMA((1,)),
         ],

time: 53.9 us -> 53.1 us (0.985)
  Pallas kernels: 53.1 us -> 52.3 us
    pallas_call x1, Pallas kernels: 41.1 us -> 40.3 us  [on_device(): pl.pallas_call(functools.partial(exchange_kernel, groups, capacity), out_...]
where the time goes in v5:
time: 53.1 us; the launch traced here: 52.9 us
  Pallas kernels  52.3 us (98%)
  between operations  0.64 us (1%)
    pallas_call x1, Pallas kernels, on_device(): pl.pallas_call(functools.partial(exchange_kernel, groups, capacity), out_...  40.3 us
    pallas_call x1, Pallas kernels, on_device(): pl.pallas_call(weight_grad_kernel, out_shape=(jax.ShapeDtypeStruct((token...  12 us

profile of v5, /device:TPU:0, one launch (start us, length us, event | category | flops | bytes accessed | tf_op | source)
XLA Modules:
  0.0 52.9 jit_solution(6706200998630965281)
XLA Ops:
  0.6 40.3 %shard_map.94 = (bf16[64,4096]{1,0:T(8,128)(2,1)S(1)}, bf16[512,4096]{1,0:T(8,128)(2,1)S(1)}, bf16[512,1024]{1,0:T(8,128)(2,1)S(1)}, bf16[512,1024]{1,0:T(8,128)(2,1)S(1)}, bf16[64,24]{1,0:T(8,128)(2,1)S(1)}) custom-call(s32[2,24]{1,0:T(2,128)} %bitcast.1, bf16[24,4096]{1,0:T(8,128)(2,1)} %tokens.1, bf16[1,4096,1024]{2,1,0:T(8,128)(2,1)} %weight_gate.1, ...), custom_call_target="tpu_custom_call" | custom-call | tf_op jit(solution)/shard_map/pallas_call | solution.py:478
  40.9 12.0 %shard_map.95 = (bf16[24,4096]{1,0:T(8,128)(2,1)}, f32[1,4096,1024]{2,1,0:T(8,128)}, f32[1,4096,1024]{2,1,0:T(8,128)}) custom-call(bf16[64,4096]{1,0:T(8,128)(2,1)S(1)} %get-tuple-element.8.returned, bf16[512,4096]{1,0:T(8,128)(2,1)S(1)} %get-tuple-element.9.block_rows, bf16[512,1024]{1,0:T(8,128)(2,1)S(1)} %get-tuple-element.10.gate_rows, ...), custom_call_target="tpu_custom_call" | custom-call | tf_op jit(solution)/shard_map/pallas_call | solution.py:516
